TPU v7x, 32 devices: a whole 2x2x4 slice. The times are simulated.
32 devices in a mesh: ctx: 16 (over z, y, x), head: 2 (over core).
Axes of the slice: x: 2, y: 2, z: 4, core: 2. Of those that a mesh axis runs over, the one named last changes fastest.
Arguments:
- hidden: bfloat16 [256, 8192], P(None, 'ctx'), may hold values from -6 to 6
- q_weight: bfloat16 [8192, 8192], P('ctx', 'head'), may hold values from -0.0625 to 0.0625
- keys: bfloat16 [8, 32768, 128], P('head', 'ctx'), may hold values from -400 to 400
- values: bfloat16 [8, 32768, 128], P('head', 'ctx'), may hold values from -6 to 6
- o_weight: bfloat16 [8192, 8192], P('head', 'ctx'), may hold values from -0.0625 to 0.0625
- start: int32 [1], replicated, may hold values from 0 to 32512
Outputs:
- importance: float32 [8, 32768], P('head', 'ctx')
- mixed: bfloat16 [256, 8192], P('head', 'ctx')
All inputs are finite; a program needn't handle non-finite values.
Results may differ from a plain program's by a relative error of at most 0.035.
Values may be sent and summed in bfloat16 or wider, within the bound.
No kernel may reach another device: no remote copies, remote signals or barrier semaphores. Data moves between devices by JAX's collectives and lax.ppermute only.
A program may use at most 64 MiB of HBM per device.

v0:
```python
import jax
import jax.numpy as jnp
from jax import lax
from jax.sharding import PartitionSpec as P

NEG = -1e30


def merged(part, axis, combine):
    gathered = jax.tree.map(lambda a: lax.all_gather(a, axis), part)

    def take(source):
        return jax.tree.map(lambda a: lax.dynamic_index_in_dim(a, source, 0, False), gathered)

    return lax.fori_loop(
        1, lax.axis_size(axis), lambda source, state: combine(state, take(source)), take(0)
    )


def combine_stats(first, second):
    peak = jnp.maximum(first[0], second[0])
    total = first[1] * jnp.exp(first[0] - peak) + second[1] * jnp.exp(second[0] - peak)
    return (peak, total)


def on_device(hidden, q_weight, keys, values, o_weight, start):
    span = hidden.shape[0]
    kv_local, s_dev, head_size = keys.shape
    head_group = q_weight.shape[1] // (kv_local * head_size)
    block_rows = head_group * span
    scale = head_size ** (-0.5)
    first_pos = start[0]
    partial_value = jnp.dot(hidden, q_weight, preferred_element_type=jnp.float32)
    query_rows = lax.psum(partial_value, "ctx").astype(jnp.bfloat16)
    query_rows = (
        query_rows.reshape(span, kv_local, head_group, head_size)
        .transpose(1, 2, 0, 3)
        .reshape(kv_local, block_rows, head_size)
    )
    rowpos = first_pos + jnp.tile(jnp.arange(span, dtype=jnp.int32), head_group)
    offset = lax.axis_index("ctx") * s_dev
    width = min(512, s_dev)
    count = s_dev // width
    key_blocks = keys.reshape(kv_local, count, width, head_size).transpose(1, 0, 2, 3)
    value_blocks = values.reshape(kv_local, count, width, head_size).transpose(1, 0, 2, 3)
    blocks = jnp.arange(count, dtype=jnp.int32)

    def scores_of(kblk, b):
        s = jnp.einsum("hrd,hkd->hrk", query_rows, kblk, preferred_element_type=jnp.float32) * scale
        keypos = offset + b * width + jnp.arange(width, dtype=jnp.int32)
        return (s, keypos[None, None, :] <= rowpos[None, :, None])

    def first(carry, item):
        kblk, b = item
        s, mask = scores_of(kblk, b)
        newm = jnp.maximum(carry[0], jnp.max(jnp.where(mask, s, NEG), axis=2))
        total = carry[1] * jnp.exp(carry[0] - newm) + jnp.sum(
            jnp.where(mask, jnp.exp(s - newm[:, :, None]), 0.0), axis=2
        )
        out = (newm, total)
        return (out, None)

    init = (
        jnp.full((kv_local, block_rows), NEG, jnp.float32),
        jnp.zeros((kv_local, block_rows), jnp.float32),
    )
    (local_peak, local_total), _ = lax.scan(first, init, (key_blocks, blocks))
    peak, total = merged((local_peak, local_total), "ctx", combine_stats)

    def second(running_total, item):
        kblk, vblk, b = item
        state = running_total
        s, mask = scores_of(kblk, b)
        prob = jnp.where(mask, jnp.exp(s - peak[:, :, None]) / total[:, :, None], 0.0)
        state = state + jnp.einsum(
            "hrk,hkd->hrd", prob.astype(jnp.bfloat16), vblk, preferred_element_type=jnp.float32
        )
        return (state, jnp.max(prob, axis=1))

    running_total, imp = lax.scan(
        second,
        jnp.zeros((kv_local, block_rows, head_size), jnp.float32),
        (key_blocks, value_blocks, blocks),
    )
    importance = (first_pos + span).astype(jnp.float32) * imp.transpose(1, 0, 2).reshape(
        kv_local, s_dev
    )
    attended_weight = lax.psum(running_total, "ctx").astype(jnp.bfloat16)
    attended_weight = (
        attended_weight.reshape(kv_local, head_group, span, head_size)
        .transpose(2, 0, 1, 3)
        .reshape(span, kv_local * head_group * head_size)
    )
    mixed = lax.psum_scatter(
        jnp.dot(attended_weight, o_weight, preferred_element_type=jnp.float32).astype(jnp.bfloat16),
        "head",
        scatter_dimension=0,
        tiled=True,
    )
    return (importance, mixed)


def solution(mesh):
    return jax.shard_map(
        on_device,
        mesh=mesh,
        in_specs=(
            P(None, "ctx"),
            P("ctx", "head"),
            P("head", "ctx", None),
            P("head", "ctx", None),
            P("head", "ctx"),
            P(),
        ),
        out_specs=(P("head", "ctx"), P("head", "ctx")),
        check_vma=False,
    )
```

profile of v0, /device:TPU:0, one launch (start us, length us, event | category | flops | bytes accessed | tf_op | source)
XLA Modules:
  0.0 638.1 jit_solution(15848075958493927574)
XLA Ops:
  7.3 0.9 copy-done
  8.1 5.4 fusion.26
  13.5 186.6 %all-reduce.2 = bf16[256,4096]{1,0:T(8,128)(2,1)S(1)} all-reduce(f32[256,4096]{1,0:T(8,128)} %fusion.26), channel_id=1, replica_groups=mesh['ctx'=16,'head'=2] {'ctx'}, use_global_device_ids=true, to_apply=%region_0.0 | all-reduce | flops 1048576 | bytes 6291456 | tf_op jit(solution)/shard_map/psum | solution.py:34
  200.6 0.8 copy.25
  201.7 1.5 copy.27
  203.2 75.7 %while.44 = (s32[]{:T(128)}, f32[4,2048]{1,0:T(4,128)S(1)}, f32[4,2048]{1,0:T(4,128)S(1)}, s32[4]{0:T(128)S(1)}, s32[]{:T(128)}, /*index=5*/bf16[4,4,512,128]{3,...) while((s32[]{:T(128)}, f32[4,2048]{1,0:T(4,128)S(1)}, ...), condition=%wide.region_4.5_spmd.clone, body=%wide.region_1.4_spmd.clone.sunk | while | flops 1104194048 | bytes 39785120 | solution.py:67
  203.2 0.7 dynamic_slice.79
  204.5 0.7 add_bitcast_fusion.4
  205.2 0.7 broadcast_compare_fusion.4
  205.9 8.4 %fusion.45 = (f32[4,2048]{1,0:T(4,128)S(1)}, f32[4,512,2048]{2,1,0:T(8,128)}) fusion(pred[2048,512]{0,1:T(8,128)(4,1)S(1)} %broadcast_compare_fusion.4, bf16[4,2048,128]{2,1,0:T(8,128)(2,1)S(1)} %get-tuple-element.611, bf16[4,4,512,128]{3,2,1,0:T(8,128)(2,1)} %get-tuple-element.610, s32[]{:T(128)} %get-tuple-element.594), kind=kOutput, calls=%fused_computation.9.clone.1 | convolution fusion | flops 1086316544 | bytes 20480512 | tf_op jit(solution)/shard_map/while/body/eval_jaxpr/hrd,hkd->hrk/dot_general | solution.py:49
  214.3 7.8 %fusion.46 = f32[4,2048]{1,0:T(4,128)S(1)} fusion(f32[4,512,2048]{2,1,0:T(8,128)} %get-tuple-element.569, f32[4,2048]{1,0:T(4,128)S(1)} %select_maximum_fusion.2, pred[2048,512]{0,1:T(8,128)(4,1)S(1)} %broadcast_compare_fusion.4), kind=kLoop, calls=%fused_computation.12.clone.1 | loop fusion | flops 16769024 | bytes 17891328 | tf_op jit(solution)/shard_map/while/body/eval_jaxpr/reduce_sum | solution.py:57
  222.1 0.7 dynamic_slice.79
  223.5 0.7 add_bitcast_fusion.4
  224.1 0.7 broadcast_compare_fusion.4
  224.8 8.4 %fusion.45 = (f32[4,2048]{1,0:T(4,128)S(1)}, f32[4,512,2048]{2,1,0:T(8,128)}) fusion(pred[2048,512]{0,1:T(8,128)(4,1)S(1)} %broadcast_compare_fusion.4, bf16[4,2048,128]{2,1,0:T(8,128)(2,1)S(1)} %get-tuple-element.611, bf16[4,4,512,128]{3,2,1,0:T(8,128)(2,1)} %get-tuple-element.610, s32[]{:T(128)} %get-tuple-element.594), kind=kOutput, calls=%fused_computation.9.clone.1 | convolution fusion | flops 1086316544 | bytes 20480512 | tf_op jit(solution)/shard_map/while/body/eval_jaxpr/hrd,hkd->hrk/dot_general | solution.py:49
  233.2 7.8 %fusion.46 = f32[4,2048]{1,0:T(4,128)S(1)} fusion(f32[4,512,2048]{2,1,0:T(8,128)} %get-tuple-element.569, f32[4,2048]{1,0:T(4,128)S(1)} %select_maximum_fusion.2, pred[2048,512]{0,1:T(8,128)(4,1)S(1)} %broadcast_compare_fusion.4), kind=kLoop, calls=%fused_computation.12.clone.1 | loop fusion | flops 16769024 | bytes 17891328 | tf_op jit(solution)/shard_map/while/body/eval_jaxpr/reduce_sum | solution.py:57
  241.0 0.7 dynamic_slice.79
  242.4 0.7 add_bitcast_fusion.4
  243.7 8.4 %fusion.45 = (f32[4,2048]{1,0:T(4,128)S(1)}, f32[4,512,2048]{2,1,0:T(8,128)}) fusion(pred[2048,512]{0,1:T(8,128)(4,1)S(1)} %broadcast_compare_fusion.4, bf16[4,2048,128]{2,1,0:T(8,128)(2,1)S(1)} %get-tuple-element.611, bf16[4,4,512,128]{3,2,1,0:T(8,128)(2,1)} %get-tuple-element.610, s32[]{:T(128)} %get-tuple-element.594), kind=kOutput, calls=%fused_computation.9.clone.1 | convolution fusion | flops 1086316544 | bytes 20480512 | tf_op jit(solution)/shard_map/while/body/eval_jaxpr/hrd,hkd->hrk/dot_general | solution.py:49
  252.1 7.8 %fusion.46 = f32[4,2048]{1,0:T(4,128)S(1)} fusion(f32[4,512,2048]{2,1,0:T(8,128)} %get-tuple-element.569, f32[4,2048]{1,0:T(4,128)S(1)} %select_maximum_fusion.2, pred[2048,512]{0,1:T(8,128)(4,1)S(1)} %broadcast_compare_fusion.4), kind=kLoop, calls=%fused_computation.12.clone.1 | loop fusion | flops 16769024 | bytes 17891328 | tf_op jit(solution)/shard_map/while/body/eval_jaxpr/reduce_sum | solution.py:57
  259.9 0.7 dynamic_slice.79
  261.3 0.7 add_bitcast_fusion.4
  262.6 8.4 %fusion.45 = (f32[4,2048]{1,0:T(4,128)S(1)}, f32[4,512,2048]{2,1,0:T(8,128)}) fusion(pred[2048,512]{0,1:T(8,128)(4,1)S(1)} %broadcast_compare_fusion.4, bf16[4,2048,128]{2,1,0:T(8,128)(2,1)S(1)} %get-tuple-element.611, bf16[4,4,512,128]{3,2,1,0:T(8,128)(2,1)} %get-tuple-element.610, s32[]{:T(128)} %get-tuple-element.594), kind=kOutput, calls=%fused_computation.9.clone.1 | convolution fusion | flops 1086316544 | bytes 20480512 | tf_op jit(solution)/shard_map/while/body/eval_jaxpr/hrd,hkd->hrk/dot_general | solution.py:49
  271.0 7.8 %fusion.46 = f32[4,2048]{1,0:T(4,128)S(1)} fusion(f32[4,512,2048]{2,1,0:T(8,128)} %get-tuple-element.569, f32[4,2048]{1,0:T(4,128)S(1)} %select_maximum_fusion.2, pred[2048,512]{0,1:T(8,128)(4,1)S(1)} %broadcast_compare_fusion.4), kind=kLoop, calls=%fused_computation.12.clone.1 | loop fusion | flops 16769024 | bytes 17891328 | tf_op jit(solution)/shard_map/while/body/eval_jaxpr/reduce_sum | solution.py:57
  278.8 42.2 %all-gather.3 = f32[16,4,2048]{2,1,0:T(4,128)S(1)} all-gather(f32[1,4,2048]{2,1,0:T(4,128)S(1)} %bitcast.128), channel_id=3, replica_groups=mesh['ctx'=16,'head'=2] {'ctx'}, dimensions={0}, use_global_device_ids=true | all-gather | bytes 557056 | tf_op jit(solution)/shard_map/all_gather | solution.py:10
  321.0 38.7 %all-gather.2 = f32[16,4,2048]{2,1,0:T(4,128)S(1)} all-gather(f32[1,4,2048]{2,1,0:T(4,128)S(1)} %bitcast.124), channel_id=2, replica_groups=mesh['ctx'=16,'head'=2] {'ctx'}, dimensions={0}, use_global_device_ids=true | all-gather | bytes 557056 | tf_op jit(solution)/shard_map/all_gather | solution.py:10
  359.8 0.8 copy-done.2
  360.6 12.4 %while.43 = (s32[]{:T(128)}, f32[4,2048]{1,0:T(4,128)S(1)}, f32[4,2048]{1,0:T(4,128)S(1)}, f32[16,4,2048]{2,1,0:T(4,128)}, f32[16,4,2048]{2,1,0:T(4,128)S(1)}, /*index=5*/s32[]{:T(128)}, s32[]{:T(128)}, s32[]{:T(128)}) while((s32[]{:T(128)}, f32[4,2048]{1,0:T(4,128)S(1)}, f32[4,2048]{1,0:T(4,128)S(1)}, f32[16,4,2048]{2,1,0:T(4,128)}, ...), condition=%wide.region_6.7_spmd, body=%wide.region_5.6_spmd.sunk | while | flops 49157 | bytes 196739 | solution.py:15
  360.6 0.8 fusion.43
  361.4 0.8 fusion.43
  362.2 0.8 fusion.43
  363.0 0.8 fusion.43
  363.9 0.8 fusion.43
  364.7 0.8 fusion.43
  365.5 0.8 fusion.43
  366.4 0.8 fusion.43
  367.2 0.8 fusion.43
  368.0 0.8 fusion.43
  368.8 0.8 fusion.43
  369.7 0.8 fusion.43
  370.5 0.8 fusion.43
  371.3 0.8 fusion.43
  372.2 0.8 fusion.43
  373.0 82.6 %while.45 = (s32[]{:T(128)}, f32[4,2048,128]{2,1,0:T(8,128)}, f32[4,4,512]{2,1,0:T(4,128)S(1)}, s32[4]{0:T(128)S(1)}, s32[]{:T(128)}, /*index=5*/bf16[4,4,512,12...) while((s32[]{:T(128)}, f32[4,2048,128]{2,1,0:T(8,128)}, ...), condition=%wide.region_9.10_spmd.clone, body=%wide.region_7.9_spmd.clone.sunk | while | flops 2175795712 | bytes 30536892 | solution.py:80
  373.0 0.7 dynamic_slice.82
  374.4 0.7 add_bitcast_fusion.5
  375.7 8.8 %fusion.51 = (f32[4,512]{1,0:T(4,128)S(1)}, bf16[4,2048,512]{1,2,0:T(8,128)(2,1)}) fusion(f32[4,2048]{1,0:T(4,128)S(1)} %get-tuple-element.676, f32[4,2048]{1,0:T(4,128)S(1)} %get-tuple-element.675, bf16[4,2048,128]{2,1,0:T(8,128)(2,1)S(1)} %get-tuple-element.674, bf16[4,4,512,128]{3,2,1,0:T(8,128)(2,1)} %get-tuple-element.673, ...), kind=kOutput, calls=%fused_computation.42.clone.1 | convolution fusion | flops 1098905600 | bytes 12132864 | tf_op jit(solution)/shard_map/while/body/eval_jaxpr/hrd,hkd->hrk/dot_general | solution.py:49
  384.5 8.1 %select_add_fusion.2 = f32[4,2048,128]{2,1,0:T(8,128)} fusion(f32[4,2048,128]{2,1,0:T(8,128)} %get-tuple-element.655, bf16[4,2048,512]{1,2,0:T(8,128)(2,1)} %get-tuple-element.581, pred[]{:T(512)S(6)} %compare.7, bf16[4,4,512,128]{3,2,0,1:T(8,128)(2,1)} %get-tuple-element.677, s32[]{:T(128)} %get-tuple-element.654), kind=kOutput, calls=%fused_computation.26.clone.1 | convolution fusion | flops 1075838976 | bytes 17302016 | tf_op jit(solution)/shard_map/while/body/eval_jaxpr/hrk,hkd->hrd/dot_general | solution.py:75
  392.7 0.7 dynamic_slice.82
  394.0 0.7 add_bitcast_fusion.5
  395.4 8.8 %fusion.51 = (f32[4,512]{1,0:T(4,128)S(1)}, bf16[4,2048,512]{1,2,0:T(8,128)(2,1)}) fusion(f32[4,2048]{1,0:T(4,128)S(1)} %get-tuple-element.676, f32[4,2048]{1,0:T(4,128)S(1)} %get-tuple-element.675, bf16[4,2048,128]{2,1,0:T(8,128)(2,1)S(1)} %get-tuple-element.674, bf16[4,4,512,128]{3,2,1,0:T(8,128)(2,1)} %get-tuple-element.673, ...), kind=kOutput, calls=%fused_computation.42.clone.1 | convolution fusion | flops 1098905600 | bytes 12132864 | tf_op jit(solution)/shard_map/while/body/eval_jaxpr/hrd,hkd->hrk/dot_general | solution.py:49
  404.2 9.4 %select_add_fusion.2 = f32[4,2048,128]{2,1,0:T(8,128)} fusion(f32[4,2048,128]{2,1,0:T(8,128)} %get-tuple-element.655, bf16[4,2048,512]{1,2,0:T(8,128)(2,1)} %get-tuple-element.581, pred[]{:T(512)S(6)} %compare.7, bf16[4,4,512,128]{3,2,0,1:T(8,128)(2,1)} %get-tuple-element.677, s32[]{:T(128)} %get-tuple-element.654), kind=kOutput, calls=%fused_computation.26.clone.1 | convolution fusion | flops 1075838976 | bytes 17302016 | tf_op jit(solution)/shard_map/while/body/eval_jaxpr/hrk,hkd->hrd/dot_general | solution.py:75
  413.6 0.7 dynamic_slice.82
  415.0 0.7 add_bitcast_fusion.5
  416.3 8.8 %fusion.51 = (f32[4,512]{1,0:T(4,128)S(1)}, bf16[4,2048,512]{1,2,0:T(8,128)(2,1)}) fusion(f32[4,2048]{1,0:T(4,128)S(1)} %get-tuple-element.676, f32[4,2048]{1,0:T(4,128)S(1)} %get-tuple-element.675, bf16[4,2048,128]{2,1,0:T(8,128)(2,1)S(1)} %get-tuple-element.674, bf16[4,4,512,128]{3,2,1,0:T(8,128)(2,1)} %get-tuple-element.673, ...), kind=kOutput, calls=%fused_computation.42.clone.1 | convolution fusion | flops 1098905600 | bytes 12132864 | tf_op jit(solution)/shard_map/while/body/eval_jaxpr/hrd,hkd->hrk/dot_general | solution.py:49
  425.1 9.4 %select_add_fusion.2 = f32[4,2048,128]{2,1,0:T(8,128)} fusion(f32[4,2048,128]{2,1,0:T(8,128)} %get-tuple-element.655, bf16[4,2048,512]{1,2,0:T(8,128)(2,1)} %get-tuple-element.581, pred[]{:T(512)S(6)} %compare.7, bf16[4,4,512,128]{3,2,0,1:T(8,128)(2,1)} %get-tuple-element.677, s32[]{:T(128)} %get-tuple-element.654), kind=kOutput, calls=%fused_computation.26.clone.1 | convolution fusion | flops 1075838976 | bytes 17302016 | tf_op jit(solution)/shard_map/while/body/eval_jaxpr/hrk,hkd->hrd/dot_general | solution.py:75
  434.6 0.7 dynamic_slice.82
  436.0 0.7 add_bitcast_fusion.5
  437.3 8.8 %fusion.51 = (f32[4,512]{1,0:T(4,128)S(1)}, bf16[4,2048,512]{1,2,0:T(8,128)(2,1)}) fusion(f32[4,2048]{1,0:T(4,128)S(1)} %get-tuple-element.676, f32[4,2048]{1,0:T(4,128)S(1)} %get-tuple-element.675, bf16[4,2048,128]{2,1,0:T(8,128)(2,1)S(1)} %get-tuple-element.674, bf16[4,4,512,128]{3,2,1,0:T(8,128)(2,1)} %get-tuple-element.673, ...), kind=kOutput, calls=%fused_computation.42.clone.1 | convolution fusion | flops 1098905600 | bytes 12132864 | tf_op jit(solution)/shard_map/while/body/eval_jaxpr/hrd,hkd->hrk/dot_general | solution.py:49
  446.1 9.4 %select_add_fusion.2 = f32[4,2048,128]{2,1,0:T(8,128)} fusion(f32[4,2048,128]{2,1,0:T(8,128)} %get-tuple-element.655, bf16[4,2048,512]{1,2,0:T(8,128)(2,1)} %get-tuple-element.581, pred[]{:T(512)S(6)} %compare.7, bf16[4,4,512,128]{3,2,0,1:T(8,128)(2,1)} %get-tuple-element.677, s32[]{:T(128)} %get-tuple-element.654), kind=kOutput, calls=%fused_computation.26.clone.1 | convolution fusion | flops 1075838976 | bytes 17302016 | tf_op jit(solution)/shard_map/while/body/eval_jaxpr/hrk,hkd->hrd/dot_general | solution.py:75
  455.5 162.3 %all-reduce.3 = bf16[4,2048,128]{2,1,0:T(8,128)(2,1)S(1)} all-reduce(f32[4,2048,128]{2,1,0:T(8,128)} %get-tuple-element.241), channel_id=1, replica_groups=mesh['ctx'=16,'head'=2] {'ctx'}, use_global_device_ids=true, to_apply=%region_10.11 | all-reduce | flops 1048576 | bytes 6291456 | tf_op jit(solution)/shard_map/psum | solution.py:88
  617.9 2.6 copy.30
  620.5 4.8 convolution_convert_fusion
  626.7 4.6 reduce-scatter.2.cloned.1.call-done
  (54 shorter events, 5.7 us)
Async XLA Ops:
  7.2 1.0 copy-start
  7.2 624.1 %reduce-scatter.2.cloned.1.call-start = ((), (), s32[]{:S(2)}) async-start(), calls=%async_computation.1 | async-start | bytes 393216 | tf_op jit(solution)/shard_map/reduce_scatter | solution.py:94
  200.1 1.6 copy-start.1
  359.8 0.8 copy-start.2
Sparse Core Ops, SparseCore 0:
  625.5 5.7 reduce-scatter.1
where the time goes:
time: 640 us; the launch traced here: 638 us
  blocking collectives  430 us (67%)
  matrix products  115 us (18%)
  other arithmetic  54.6 us (9%)
  between operations  14.8 us (2%)
  local copies, waits for them, and re-layouts  12.8 us (2%)
    psum x1, blocking collectives, on_device(): query_rows = lax.psum(partial_value, 'ctx').astype(jnp.bfloat16)  187 us
    psum x1, blocking collectives, on_device(): attended_weight = lax.psum(running_total, 'ctx').astype(jnp.bfloat16)  162 us
    all_gather x2, blocking collectives, merged(): gathered = jax.tree.map(lambda a: lax.all_gather(a, axis), part)  80.9 us
    dot_general x8, matrix products, scores_of(): jnp.einsum('hrd,hkd->hrk', query_rows, kblk, preferred_element_type=jnp.f...  68.7 us
    dot_general x4, matrix products, second(): jnp.einsum('hrk,hkd->hrd', prob.astype(jnp.bfloat16), vblk, preferred_ele...  36.5 us
    reduce_sum x4, other arithmetic, first(): jnp.sum(jnp.where(mask, jnp.exp(s - newm[:, :, None]), 0.0), axis=2)  31 us
  transfers between devices with their start and end apart: 1, of which 1 were waited for; matrix products, arithmetic and copies ran while one was open for 0% of the time, Pallas kernels for 0%

commit v1 on v0

v1 whole, which is shorter than its diff:
```python
import functools
import math

import jax
import jax.numpy as jnp
from jax import lax
from jax.experimental import pallas as pl
from jax.experimental.pallas import tpu as pltpu
from jax.sharding import PartitionSpec as P

NEG = -1e30
BF = jnp.bfloat16
F32 = jnp.float32
LANES = 128


def digits_of(n):
    out, shift = [], 0
    while n > 1:
        r = 4 if n % 4 == 0 else 2
        out.append((r, shift))
        n //= r
        shift += r.bit_length() - 1
    return out


def swap(x, axis, v):
    n = lax.axis_size(axis)
    return lax.ppermute(x, axis, [(i, i ^ v) for i in range(n)])


def block_order(digits):
    order = [0]
    for r, shift in reversed(digits):
        order = [(v << shift) | o for v in range(r) for o in order]
    return order


def gather_rows(x, axis, digits, base):
    for r, shift in reversed(digits):
        x = jnp.concatenate([x] + [swap(x, axis, v << (shift + base)) for v in range(1, r)])
    return x


def permuted_rows(x, index, order):
    blocks = x.reshape(len(order), x.shape[0] // len(order), x.shape[1])
    return jnp.concatenate(
        [lax.dynamic_index_in_dim(blocks, index ^ o, 0, False) for o in order]
    )


def cdot(a, b, ca, cb):
    return lax.dot_general(a, b, (((ca,), (cb,)), ((), ())), preferred_element_type=F32)


def project_kernel(s_ref, h_ref, w_ref, o_ref):
    o_ref[...] = jnp.dot(h_ref[...], w_ref[...], preferred_element_type=F32).astype(o_ref.dtype)


def project(block, hidden, weight, width, dtype):
    rows, k = hidden.shape
    return pl.pallas_call(
        project_kernel,
        out_shape=jax.ShapeDtypeStruct((rows, width), dtype),
        grid_spec=pltpu.PrefetchScalarGridSpec(
            num_scalar_prefetch=1,
            grid=(1,),
            in_specs=[
                pl.BlockSpec((rows, k), lambda i, s: (0, 0)),
                pl.BlockSpec((k, width), lambda i, s: (0, s[0])),
            ],
            out_specs=pl.BlockSpec((rows, width), lambda i, s: (0, 0)),
        ),
        name="query_projection",
    )(block, hidden, weight)


def visible(s, base, limit_ref):
    pos = lax.broadcasted_iota(jnp.int32, s.shape, 0) + base
    return jnp.where(pos <= limit_ref[0:1, :], s, NEG)


def attend_kernel(n_src, per, bk, span, c, s_ref, q_ref, lim_ref, *refs):
    ks, vs = refs[:n_src], refs[n_src : 2 * n_src]
    o_ref, acc, peak, stat = refs[2 * n_src :]
    d = LANES
    heads = q_ref.shape[1] // d
    ones = jnp.ones((16, bk), BF)

    for first in range(0, heads, per):
        for j in range(per):
            acc[j] = jnp.zeros(acc.shape[1:], F32)
            peak[j] = jnp.full(peak.shape[1:], NEG, F32)

        def block(src, kb, masked):
            k = ks[src][pl.ds(pl.multiple_of(kb * bk, bk), bk), :]
            vt = jnp.concatenate([vs[src][kb], ones])
            for j in range(per):
                g = first + j
                s = cdot(k, q_ref[:, g * d : (g + 1) * d], 1, 1)
                if masked:
                    s = visible(s, s_ref[2 * n_src + src] + kb * bk, lim_ref)
                old = peak[j, 0:1, :]
                new = jnp.maximum(old, jnp.max(s, axis=0, keepdims=True))
                p = jnp.exp2((s - new) * c).astype(BF)
                acc[j] = acc[j] * jnp.exp2((old - new) * c) + cdot(vt, p, 1, 0)
                peak[j, 0:1, :] = new

        for src in range(n_src):
            full, some = s_ref[src], s_ref[n_src + src]
            lax.fori_loop(0, full, lambda kb, x: (block(src, kb, False), x)[1], 0)
            lax.fori_loop(full, some, lambda kb, x: (block(src, kb, True), x)[1], 0)

        for j in range(per):
            g = first + j
            total = jnp.maximum(acc[j, d : d + 1, :], 1e-30)
            out = acc[j, 0:d, :] / total
            o_ref[:, g * d : (g + 1) * d] = out.T.astype(BF)
            stat[g : g + 1, :] = peak[j, 0:1, :] * c + jnp.log2(total)

    level = stat[...]
    hi = level.astype(BF).astype(F32)
    mid = (level - hi).astype(BF).astype(F32)
    low = level - hi - mid
    pad = jnp.zeros((d - 3 * heads, span), F32)
    o_ref[:, heads * d : (heads + 1) * d] = jnp.concatenate([hi, mid, low, pad]).T.astype(BF)


def attend(scal, q, limit, ks, vs, bk, c):
    span, width = q.shape
    heads, n_src = width // LANES, len(ks)
    per = min(4, heads)
    keys = ks[0].shape[0] * n_src
    vm = pl.BlockSpec(memory_space=pltpu.VMEM)
    return pl.pallas_call(
        functools.partial(attend_kernel, n_src, per, bk, span, c),
        out_shape=jax.ShapeDtypeStruct((span, width + LANES), BF),
        in_specs=[pl.BlockSpec(memory_space=pltpu.SMEM)] + [vm] * (2 + 2 * n_src),
        out_specs=vm,
        scratch_shapes=[
            pltpu.VMEM((per, LANES + 16, span), F32),
            pltpu.VMEM((per, 8, span), F32),
            pltpu.VMEM((heads, span), F32),
        ],
        cost_estimate=pl.CostEstimate(
            flops=4 * span * heads * LANES * keys,
            transcendentals=span * heads * keys,
            bytes_accessed=2 * span * width * 2 + 4 * keys * LANES,
        ),
        name="attend",
    )(scal, q, limit, *ks, *vs)


def merge_kernel(heads, *refs):
    srcs, o_ref = refs[:-1], refs[-1]
    d = LANES

    def level_of(r):
        parts = r[:, heads * d : (heads + 1) * d].astype(F32)
        return parts + pltpu.roll(parts, d - heads, 1) + pltpu.roll(parts, d - 2 * heads, 1)

    levels = [level_of(r) for r in srcs]
    top = functools.reduce(jnp.maximum, levels)
    weights = [jnp.exp2(x - top) for x in levels]
    total = functools.reduce(jnp.add, weights)
    weights = [w / total for w in weights]
    for g in range(heads):
        o_ref[:, g * d : (g + 1) * d] = functools.reduce(
            jnp.add,
            [w[:, g : g + 1] * r[:, g * d : (g + 1) * d].astype(F32) for w, r in zip(weights, srcs)],
        ).astype(BF)
    level = top + jnp.log2(total)
    lane = lax.broadcasted_iota(jnp.int32, level.shape, 1)
    level = jnp.where(lane < heads, level, 0.0)
    hi = level.astype(BF).astype(F32)
    mid = (level - hi).astype(BF).astype(F32)
    low = level - hi - mid
    o_ref[:, heads * d : (heads + 1) * d] = (
        hi + pltpu.roll(mid, heads, 1) + pltpu.roll(low, 2 * heads, 1)
    ).astype(BF)


def merge(parts):
    shape = parts[0].shape
    return pl.pallas_call(
        functools.partial(merge_kernel, shape[1] // LANES - 1),
        out_shape=jax.ShapeDtypeStruct(shape, BF),
        name="merge",
    )(*parts)


def importance_kernel(n_src, bk, c, s_ref, q_ref, a_ref, lim_ref, *refs):
    ks, o_ref, lev = refs[:n_src], refs[n_src], refs[n_src + 1]
    d = LANES
    heads = q_ref.shape[1] // d
    parts = a_ref[:, heads * d : (heads + 1) * d].astype(F32).T
    level = parts[0:heads] + parts[heads : 2 * heads] + parts[2 * heads : 3 * heads]
    lev[...] = level * (1.0 / c)
    factor = s_ref[3 * n_src].astype(F32)
    o_ref[...] = jnp.zeros(o_ref.shape, F32)

    def block(src, kb, masked):
        k = ks[src][pl.ds(pl.multiple_of(kb * bk, bk), bk), :]
        best = None
        for g in range(heads):
            s = cdot(k, q_ref[:, g * d : (g + 1) * d], 1, 1) - lev[g : g + 1, :]
            best = s if best is None else jnp.maximum(best, s)
        if masked:
            best = visible(best, s_ref[2 * n_src + src] + kb * bk, lim_ref)
        best = functools.reduce(
            jnp.maximum, [best[:, x : x + d] for x in range(0, best.shape[1], d)]
        )
        best = jnp.max(best.T, axis=0, keepdims=True)
        o_ref[src, pl.ds(kb, 1), :] = factor * jnp.exp2(best * c)

    for src in range(n_src):
        full, some = s_ref[src], s_ref[n_src + src]
        lax.fori_loop(0, full, lambda kb, x: (block(src, kb, False), x)[1], 0)
        lax.fori_loop(full, some, lambda kb, x: (block(src, kb, True), x)[1], 0)


def importance_of(scal, q, attended, limit, ks, bk, c):
    span, width = q.shape
    heads, n_src = width // LANES, len(ks)
    per_src = ks[0].shape[0]
    vm = pl.BlockSpec(memory_space=pltpu.VMEM)
    return pl.pallas_call(
        functools.partial(importance_kernel, n_src, bk, c),
        out_shape=jax.ShapeDtypeStruct((n_src, per_src // bk, bk), F32),
        in_specs=[pl.BlockSpec(memory_space=pltpu.SMEM)] + [vm] * (3 + n_src),
        out_specs=vm,
        scratch_shapes=[pltpu.VMEM((heads, span), F32)],
        cost_estimate=pl.CostEstimate(
            flops=2 * span * heads * LANES * per_src * n_src,
            transcendentals=per_src * n_src,
            bytes_accessed=2 * span * width * 2 + 2 * per_src * n_src * LANES,
        ),
        name="importance",
    )(scal, q, attended, limit, *ks)


def output_kernel(s_ref, a_ref, w_ref, c_ref, o_ref):
    o_ref[...] = c_ref[...] + jnp.dot(a_ref[...], w_ref[...], preferred_element_type=F32)


def output_kernel_first(s_ref, a_ref, w_ref, o_ref):
    o_ref[...] = jnp.dot(a_ref[...], w_ref[...], preferred_element_type=F32)


def output_part(block, attended, weight, width, carry):
    rows = attended.shape[0]
    cols = weight.shape[1]
    specs = [
        pl.BlockSpec((rows, width), lambda i, s: (0, 0)),
        pl.BlockSpec((width, cols), lambda i, s: (s[0], 0)),
    ]
    whole = pl.BlockSpec((rows, cols), lambda i, s: (0, 0))
    return pl.pallas_call(
        output_kernel_first if carry is None else output_kernel,
        out_shape=jax.ShapeDtypeStruct((rows, cols), F32),
        grid_spec=pltpu.PrefetchScalarGridSpec(
            num_scalar_prefetch=1,
            grid=(1,),
            in_specs=specs + ([] if carry is None else [whole]),
            out_specs=whole,
        ),
        name="output_projection",
    )(block, attended, weight, *([] if carry is None else [carry]))


def on_device(hidden, q_weight, keys, values, o_weight, start):
    span = hidden.shape[0]
    group, s_dev, head_size = keys.shape
    n = lax.axis_size("ctx")
    nh = lax.axis_size("head")
    width = q_weight.shape[1] // group
    scale = head_size**-0.5
    c = scale * math.log2(math.e)
    base = group.bit_length() - 1
    here = lax.axis_index("ctx")
    mine, outer = here % group, here // group
    digits = digits_of(n // group)
    order = block_order(digits)
    bk = min(512, s_dev)

    rows_here = permuted_rows(hidden, outer, order)
    row_index = permuted_rows(
        jnp.arange(span, dtype=jnp.int32)[:, None], outer, order
    ).reshape(1, span)
    limit = jnp.broadcast_to(start[0] + row_index, (8, span))

    def block_id(v):
        return (mine ^ v).astype(jnp.int32).reshape(1)

    parts = [
        project(block_id(v), rows_here, q_weight, width, BF if v else F32)
        for v in list(range(1, group)) + [0]
    ]
    got = [swap(parts[v - 1], "ctx", v) for v in range(1, group)]
    query = functools.reduce(jnp.add, [g.astype(F32) for g in got], parts[-1])

    count = s_dev // bk
    value_t = values.reshape(group, count, bk, head_size).transpose(0, 1, 3, 2)
    k_own = lax.dynamic_index_in_dim(keys, mine, 0, False)
    v_own = lax.dynamic_index_in_dim(value_t, mine, 0, False)
    sends = [lax.dynamic_index_in_dim(keys, mine ^ v, 0, False) for v in range(1, group)]
    vsends = [lax.dynamic_index_in_dim(value_t, mine ^ v, 0, False) for v in range(1, group)]
    query, sends, vsends = lax.optimization_barrier((query, sends, vsends))
    ks = [k_own] + [swap(x, "ctx", v + 1) for v, x in enumerate(sends)]
    vs = [v_own] + [swap(x, "ctx", v + 1) for v, x in enumerate(vsends)]

    for r, shift in digits:
        pieces = jnp.split(query, r)
        got = [swap(pieces[v].astype(BF), "ctx", v << (shift + base)) for v in range(1, r)]
        query = functools.reduce(jnp.add, [g.astype(F32) for g in got], pieces[0])
    query = gather_rows(query.astype(BF), "ctx", digits, base)

    offsets = jnp.stack([(here ^ v) * s_dev for v in range(group)]).astype(jnp.int32)
    reach = start[0] - offsets
    full = jnp.clip((reach + 1) // bk, 0, count)
    some = jnp.clip((reach + span - 1) // bk + 1, 0, count)
    scal = jnp.concatenate([full, some, offsets, start + span]).astype(jnp.int32)

    part = attend(scal, query, limit, ks, vs, bk, c)
    for r, shift in digits:
        pieces = jnp.split(part, r)
        got = [swap(pieces[v], "ctx", v << (shift + base)) for v in range(1, r)]
        part = merge([pieces[0]] + got)
    attended = gather_rows(part, "ctx", digits, base)

    own = attended[:, :width]
    arrived = [own] + [swap(own, "ctx", v) for v in range(1, group)]
    scores = importance_of(scal, query, attended, limit, ks, bk, c)
    pieces = [scores[v].reshape(1, s_dev) for v in range(group)]
    pieces = [pieces[0]] + [swap(pieces[v], "ctx", v) for v in range(1, group)]
    pieces = jnp.concatenate(pieces)
    importance = (
        jnp.concatenate(
            [lax.dynamic_index_in_dim(pieces, mine ^ h, 0, True) for h in range(group)]
        )
    )

    out = None
    for v in range(group):
        out = output_part(block_id(v), arrived[v], o_weight, width, out)
    out = out.astype(BF)
    rb = span // len(order)
    place = {o: i for i, o in enumerate(order)}
    blocks = out.reshape(len(order), rb, out.shape[1])
    where = jnp.asarray([place[o] for o in range(len(order))], jnp.int32)
    out = jnp.concatenate(
        [
            lax.dynamic_index_in_dim(blocks, where[outer ^ b], 0, False)
            for b in range(len(order))
        ]
    )
    halves = out.reshape(nh, span // nh, out.shape[1])
    me = lax.axis_index("head")
    total = lax.dynamic_index_in_dim(halves, me, 0, False).astype(F32)
    for v in range(1, nh):
        total = total + swap(
            lax.dynamic_index_in_dim(halves, me ^ v, 0, False), "head", v
        ).astype(F32)
    return (importance, total.astype(BF))


def solution(mesh):
    return jax.shard_map(
        on_device,
        mesh=mesh,
        in_specs=(
            P(None, "ctx"),
            P("ctx", "head"),
            P("head", "ctx", None),
            P("head", "ctx", None),
            P("head", "ctx"),
            P(),
        ),
        out_specs=(P("head", "ctx"), P("head", "ctx")),
        check_vma=False,
    )
```

time: 640 us -> 240 us (0.38)
  blocking collectives: 430 us -> 0 us
  matrix products: 115 us -> 0 us
  Pallas kernels: 0 us -> 99.3 us
  waiting for transfers between devices: 4.66 us -> 79.6 us
  other arithmetic: 54.6 us -> 6.98 us
  starting transfers between devices: 0.04 us -> 34.7 us
  between operations: 14.8 us -> 1.54 us
    psum x2 -> x0, blocking collectives: 349 us -> none  [the longest x1 187 us: on_device(): query_rows = lax.psum(partial_value, 'ctx').astype(jnp.bfloat16)]
    dot_general x14 -> x0, matrix products: 115 us -> none  [the longest x8 68.7 us: scores_of(): jnp.einsum('hrd,hkd->hrk', query_rows, kblk, preferred_element_type=jnp.f...]
    pallas_call x0 -> x11, Pallas kernels: none -> 99.3 us  [the longest x1 60 us: attend(): pl.pallas_call(functools.partial(attend_kernel, n_src, per, bk, span, c),...]
    all_gather x2 -> x0, blocking collectives: 80.9 us -> none  [merged(): gathered = jax.tree.map(lambda a: lax.all_gather(a, axis), part)]
    ppermute x0 -> x28, waiting for transfers between devices: none -> 79.6 us  [swap(): return lax.ppermute(x, axis, [(i, i ^ v) for i in range(n)])]
    ppermute x0 -> x28, starting transfers between devices: none -> 34.7 us  [swap(): return lax.ppermute(x, axis, [(i, i ^ v) for i in range(n)])]
    reduce_sum x4 -> x0, other arithmetic: 31 us -> none  [first(): jnp.sum(jnp.where(mask, jnp.exp(s - newm[:, :, None]), 0.0), axis=2)]
    add x27 -> x2, other arithmetic: 12.5 us -> 1.76 us  [the longest x1 1.68 us: on_device(): query = functools.reduce(jnp.add, [g.astype(F32) for g in got], parts[-1])]
  transfers between devices with their start and end apart: 1 -> 28, of which waited for: 1 -> 17; matrix products, arithmetic and copies ran while one was open for 0% -> 5% of each run, Pallas kernels for 0% -> 13%
where the time goes in v1:
time: 240 us; the launch traced here: 239 us
  Pallas kernels  99.3 us (41%)
  waiting for transfers between devices  79.6 us (33%)
  starting transfers between devices  34.7 us (14%)
  local copies, waits for them, and re-layouts  16.9 us (7%)
  other arithmetic  6.98 us (3%)
    ppermute x28, waiting for transfers between devices, swap(): return lax.ppermute(x, axis, [(i, i ^ v) for i in range(n)])  79.6 us
    pallas_call x1, Pallas kernels, attend(): pl.pallas_call(functools.partial(attend_kernel, n_src, per, bk, span, c),...  60 us
    ppermute x28, starting transfers between devices, swap(): return lax.ppermute(x, axis, [(i, i ^ v) for i in range(n)])  34.7 us
    pallas_call x1, Pallas kernels, importance_of(): pl.pallas_call(functools.partial(importance_kernel, n_src, bk, c), out_sh...  15.5 us
    pallas_call x4, Pallas kernels, output_part(): pl.pallas_call(output_kernel_first if carry is None else output_kernel, o...  10.9 us
    pallas_call x4, Pallas kernels, project(): pl.pallas_call(project_kernel, out_shape=jax.ShapeDtypeStruct((rows, widt...  10.5 us
    unnamed x37, local copies, waits for them, and re-layouts  10.3 us
  transfers between devices with their start and end apart: 28, of which 17 were waited for; matrix products, arithmetic and copies ran while one was open for 5% of the time, Pallas kernels for 13%

profile of v1, /device:TPU:0, one launch (start us, length us, event | category | flops | bytes accessed | tf_op | source)
XLA Modules:
  0.0 238.9 jit_solution(2415037022496830948)
XLA Ops:
  0.7 1.0 dynamic-slice_bitcast_fusion.12
  1.6 0.7 pad_maximum_fusion.2.h_ref
  2.4 2.5 %query_projection.5 = bf16[256,1024]{1,0:T(8,128)(2,1)} custom-call(s32[1]{0:T(128)} %bitcast.11.s_ref, bf16[256,512]{1,0:T(8,128)(2,1)} %pad_maximum_fusion.2.h_ref, bf16[512,4096]{1,0:T(8,128)(2,1)} %w_ref.11), custom_call_target="tpu_custom_call" | custom-call | tf_op jit(solution)/shard_map/query_projection/pallas_call | solution.py:62
  4.9 3.0 %collective-permute-start = (bf16[256,1024]{1,0:T(8,128)(2,1)}, bf16[256,1024]{1,0:T(8,128)(2,1)}, u32[]{:S(2)}, u32[]{:S(2)}) collective-permute-start(bf16[256,1024]{1,0:T(8,128)(2,1)} %query_projection.5), channel_id=1, source_target_pairs={{0,2},{2,0},{4,6},{6,4},{8,10},{10,8},{12,14},{14,12},{16,18},{18,... | collective-permute-start | bytes 1572872 | tf_op jit(solution)/shard_map/ppermute | solution.py:29
  7.9 2.5 %query_projection.6 = bf16[256,1024]{1,0:T(8,128)(2,1)} custom-call(s32[1]{0:T(128)} %bitcast.12.s_ref, bf16[256,512]{1,0:T(8,128)(2,1)} %pad_maximum_fusion.2.h_ref, bf16[512,4096]{1,0:T(8,128)(2,1)} %w_ref.11), custom_call_target="tpu_custom_call" | custom-call | tf_op jit(solution)/shard_map/query_projection/pallas_call | solution.py:62
  10.4 1.5 collective-permute-start.1
  11.9 2.6 %query_projection.7 = bf16[256,1024]{1,0:T(8,128)(2,1)} custom-call(s32[1]{0:T(128)} %bitcast.13.s_ref, bf16[256,512]{1,0:T(8,128)(2,1)} %pad_maximum_fusion.2.h_ref, bf16[512,4096]{1,0:T(8,128)(2,1)} %w_ref.11), custom_call_target="tpu_custom_call" | custom-call | tf_op jit(solution)/shard_map/query_projection/pallas_call | solution.py:62
  14.5 2.9 %query_projection.4 = f32[256,1024]{1,0:T(8,128)} custom-call(s32[1]{0:T(128)} %bitcast.5.s_ref, bf16[256,512]{1,0:T(8,128)(2,1)} %pad_maximum_fusion.2.h_ref, bf16[512,4096]{1,0:T(8,128)(2,1)} %w_ref.11), custom_call_target="tpu_custom_call" | custom-call | tf_op jit(solution)/shard_map/query_projection/pallas_call | solution.py:62
  17.4 1.2 constant_dynamic-slice_fusion.4
  18.5 2.0 copy.13
  20.6 2.2 copy.14
  22.8 1.0 copy.15
  23.8 1.2 dynamic-slice_bitcast_fusion
  25.0 10.3 %collective-permute-done.1 = bf16[256,1024]{1,0:T(8,128)(2,1)} collective-permute-done((bf16[256,1024]{1,0:T(8,128)(2,1)}, bf16[256,1024]{1,0:T(8,128)(2,1)}, u32[]{:S(2)}, u32[]{:S(2)}) %collective-permute-start.1) | collective-permute-done | bytes 524320 | tf_op jit(solution)/shard_map/ppermute | solution.py:29
  35.4 1.7 convert_add_fusion
  37.2 1.6 collective-permute-start.10
  38.8 1.6 collective-permute-start.3
  40.4 2.6 %collective-permute-start.4 = (bf16[64,1024]{1,0:T(8,128)(2,1)S(1)}, bf16[64,1024]{1,0:T(8,128)(2,1)S(1)}, u32[]{:S(2)}, u32[]{:S(2)}) collective-permute-start(bf16[64,1024]{1,0:T(8,128)(2,1)S(1)} %get-tuple-element.32), channel_id=1, source_target_pairs={{0,16},{2,18},{4,20},{6,22},{8,24},{10,26},{12,28},{14,30},{16,0},... | collective-permute-start | bytes 393224 | tf_op jit(solution)/shard_map/ppermute | solution.py:29
  43.2 1.6 collective-permute-done.3
  44.8 7.0 %collective-permute-done.4 = bf16[64,1024]{1,0:T(8,128)(2,1)S(1)} collective-permute-done((bf16[64,1024]{1,0:T(8,128)(2,1)S(1)}, bf16[64,1024]{1,0:T(8,128)(2,1)S(1)}, u32[]{:S(2)}, u32[]{:S(2)}) %collective-permute-start.4) | collective-permute-done | bytes 131104 | tf_op jit(solution)/shard_map/ppermute | solution.py:29
  52.0 2.0 collective-permute-start.6
  54.0 1.1 collective-permute-start.7
  55.1 1.4 collective-permute-start.8
  58.0 1.2 collective-permute-start.12
  59.3 5.9 %collective-permute-done.7 = bf16[64,1024]{1,0:T(8,128)(2,1)S(1)} collective-permute-done((bf16[64,1024]{1,0:T(8,128)(2,1)S(1)}, bf16[64,1024]{1,0:T(8,128)(2,1)S(1)}, u32[]{:S(2)}, u32[]{:S(2)}) %collective-permute-start.7) | collective-permute-done | bytes 131104 | tf_op jit(solution)/shard_map/ppermute | solution.py:29
  65.2 0.9 collective-permute-start.13
  66.1 1.1 collective-permute-start.14
  67.2 1.5 collective-permute-start.9
  68.7 1.0 copy.16
  69.7 0.7 concatenate.25.s_ref
  70.5 0.8 pad_maximum_fusion.1.q_ref
  71.3 2.1 collective-permute-done.11.refs_3_
  73.4 10.3 %collective-permute-done.12.refs_5_ = bf16[4,128,512]{2,1,0:T(8,128)(2,1)} collective-permute-done((bf16[4,128,512]{2,1,0:T(8,128)(2,1)S(1)}, bf16[4,128,512]{2,1,0:T(8,128)(2,1)}, u32[]{:S(2)}, u32[]{:S(2)}) %collective-permute-start.12) | collective-permute-done | bytes 524320 | tf_op jit(solution)/shard_map/ppermute | solution.py:29
  83.6 0.9 collective-permute-done.13.refs_6_
  84.5 11.3 %collective-permute-done.14.refs_7_ = bf16[4,128,512]{2,1,0:T(8,128)(2,1)} collective-permute-done((bf16[4,128,512]{2,1,0:T(8,128)(2,1)S(1)}, bf16[4,128,512]{2,1,0:T(8,128)(2,1)}, u32[]{:S(2)}, u32[]{:S(2)}) %collective-permute-start.14) | collective-permute-done | bytes 524320 | tf_op jit(solution)/shard_map/ppermute | solution.py:29
  95.8 7.4 %collective-permute-done.9.refs_1_ = bf16[2048,128]{1,0:T(8,128)(2,1)} collective-permute-done((bf16[2048,128]{1,0:T(8,128)(2,1)S(1)}, bf16[2048,128]{1,0:T(8,128)(2,1)}, u32[]{:S(2)}, u32[]{:S(2)}) %collective-permute-start.9) | collective-permute-done | bytes 524320 | tf_op jit(solution)/shard_map/ppermute | solution.py:29
  103.8 60.0 %attend.1 = bf16[256,1152]{1,0:T(8,128)(2,1)} custom-call(s32[13]{0:T(128)} %concatenate.25.s_ref, bf16[256,1024]{1,0:T(8,128)(2,1)} %pad_maximum_fusion.1.q_ref, s32[8,256]{1,0:T(8,128)} %broadcast_in_dim.2.lim_ref, bf16[2048,128]{1,0:T(8,128)(2,1)} %get-tuple-element.22.refs_0_, bf16[2048,128]{1,0:T(8,128)(2,1)} %collective-permute-done.9.refs_1_, ...), custom_call_target="tpu_custom_call" | custom-call | flops 8589934592 | bytes 5242880 | tf_op jit(solution)/shard_map/attend/pallas_call | solution.py:135
  163.9 1.8 fusion.6
  165.7 0.8 collective-permute-start.15
  166.5 3.6 %collective-permute-start.17 = (bf16[64,1152]{1,0:T(8,128)(2,1)S(1)}, bf16[64,1152]{1,0:T(8,128)(2,1)S(1)}, u32[]{:S(2)}, u32[]{:S(2)}) collective-permute-start(bf16[64,1152]{1,0:T(8,128)(2,1)S(1)} %get-tuple-element.26), channel_id=1, source_target_pairs={{0,24},{2,26},{4,28},{6,30},{8,16},{10,18},{12,20},{14,22},{16,8},... | collective-permute-start | bytes 442376 | tf_op jit(solution)/shard_map/ppermute | solution.py:29
  170.1 3.2 %collective-permute-done.15.refs_1_ = bf16[64,1152]{1,0:T(8,128)(2,1)S(1)} collective-permute-done((bf16[64,1152]{1,0:T(8,128)(2,1)S(1)}, bf16[64,1152]{1,0:T(8,128)(2,1)S(1)}, u32[]{:S(2)}, u32[]{:S(2)}) %collective-permute-start.15) | collective-permute-done | bytes 147488 | tf_op jit(solution)/shard_map/ppermute | solution.py:29
  173.2 4.0 %collective-permute-done.16.refs_2_ = bf16[64,1152]{1,0:T(8,128)(2,1)S(1)} collective-permute-done((bf16[64,1152]{1,0:T(8,128)(2,1)S(1)}, bf16[64,1152]{1,0:T(8,128)(2,1)S(1)}, u32[]{:S(2)}, u32[]{:S(2)}) %collective-permute-start.16) | collective-permute-done | bytes 147488 | tf_op jit(solution)/shard_map/ppermute | solution.py:29
  178.0 2.3 merge.1
  180.2 2.6 %collective-permute-start.18 = (bf16[64,1152]{1,0:T(8,128)(2,1)}, bf16[64,1152]{1,0:T(8,128)(2,1)S(1)}, u32[]{:S(2)}, u32[]{:S(2)}) collective-permute-start(bf16[64,1152]{1,0:T(8,128)(2,1)} %merge.1), channel_id=1, source_target_pairs={{0,8},{2,10},{4,12},{6,14},{8,0},{10,2},{12,4},{14,6},{16,24},{18,... | collective-permute-start | bytes 442376 | tf_op jit(solution)/shard_map/ppermute | solution.py:29
  182.9 2.4 collective-permute-start.20
  185.3 2.2 collective-permute-done.18
  187.5 8.0 %collective-permute-done.19 = bf16[64,1152]{1,0:T(8,128)(2,1)S(1)} collective-permute-done((bf16[64,1152]{1,0:T(8,128)(2,1)}, bf16[64,1152]{1,0:T(8,128)(2,1)S(1)}, u32[]{:S(2)}, u32[]{:S(2)}) %collective-permute-start.19) | collective-permute-done | bytes 147488 | tf_op jit(solution)/shard_map/ppermute | solution.py:29
  195.5 1.0 pad_maximum_fusion.a_ref
  197.5 2.6 %collective-permute-start.24 = (bf16[256,1024]{1,0:T(8,128)(2,1)S(1)}, bf16[256,1024]{1,0:T(8,128)(2,1)S(1)}, u32[]{:S(2)}, u32[]{:S(2)}) collective-permute-start(bf16[256,1024]{1,0:T(8,128)(2,1)S(1)} %slice.24.a_ref), channel_id=1, source_target_pairs={{0,6},{2,4},{4,2},{6,0},{8,14},{10,12},{12,10},{14,8},{16,22},{18,... | collective-permute-start | bytes 1572872 | tf_op jit(solution)/shard_map/ppermute | solution.py:29
  200.1 15.5 %importance.1 = f32[4,4,512]{2,1,0:T(4,128)} custom-call(s32[13]{0:T(128)} %concatenate.25.s_ref, bf16[256,1024]{1,0:T(8,128)(2,1)} %pad_maximum_fusion.1.q_ref, bf16[256,1152]{1,0:T(8,128)(2,1)} %copy-done.1, s32[8,256]{1,0:T(8,128)} %broadcast_in_dim.2.lim_ref, bf16[2048,128]{1,0:T(8,128)(2,1)} %get-tuple-element.22.refs_0_, ...), custom_call_target="tpu_custom_call" | custom-call | flops 4294967296 | bytes 3145728 | tf_op jit(solution)/shard_map/importance/pallas_call | solution.py:227
  215.6 0.8 slice_bitcast_fusion.3
  217.4 2.8 %collective-permute-done.21 = f32[1,2048]{1,0:T(1,128)S(1)} collective-permute-done((f32[1,2048]{1,0:T(1,128)S(1)}, f32[1,2048]{1,0:T(1,128)S(1)}, u32[]{:S(2)}, u32[]{:S(2)}) %collective-permute-start.21) | collective-permute-done | bytes 8224 | tf_op jit(solution)/shard_map/ppermute | solution.py:29
  220.5 2.6 %output_projection.4.c_ref = f32[256,512]{1,0:T(8,128)} custom-call(s32[1]{0:T(128)} %bitcast.5.s_ref, bf16[256,1024]{1,0:T(8,128)(2,1)} %copy-done.4, bf16[4096,512]{1,0:T(8,128)(2,1)} %w_ref.15), custom_call_target="tpu_custom_call" | custom-call | tf_op jit(solution)/shard_map/output_projection/pallas_call | solution.py:258
  223.2 1.6 collective-permute-done.23
  224.9 0.8 copy-done.7
  225.7 2.7 %output_projection.5.c_ref = f32[256,512]{1,0:T(8,128)} custom-call(s32[1]{0:T(128)} %bitcast.11.s_ref, bf16[256,1024]{1,0:T(8,128)(2,1)} %copy-done.7, bf16[4096,512]{1,0:T(8,128)(2,1)} %w_ref.15, f32[256,512]{1,0:T(8,128)} %output_projection.4.c_ref), custom_call_target="tpu_custom_call" | custom-call | tf_op jit(solution)/shard_map/output_projection/pallas_call | solution.py:258
  228.5 0.8 copy-done.6
  229.3 2.8 %output_projection.6.c_ref = f32[256,512]{1,0:T(8,128)} custom-call(s32[1]{0:T(128)} %bitcast.12.s_ref, bf16[256,1024]{1,0:T(8,128)(2,1)} %copy-done.6, bf16[4096,512]{1,0:T(8,128)(2,1)} %w_ref.15, f32[256,512]{1,0:T(8,128)} %output_projection.5.c_ref), custom_call_target="tpu_custom_call" | custom-call | tf_op jit(solution)/shard_map/output_projection/pallas_call | solution.py:258
  232.1 0.8 copy-done.5
  232.9 2.8 %output_projection.7 = f32[256,512]{1,0:T(8,128)} custom-call(s32[1]{0:T(128)} %bitcast.13.s_ref, bf16[256,1024]{1,0:T(8,128)(2,1)} %copy-done.5, bf16[4096,512]{1,0:T(8,128)(2,1)} %w_ref.15, f32[256,512]{1,0:T(8,128)} %output_projection.6.c_ref), custom_call_target="tpu_custom_call" | custom-call | tf_op jit(solution)/shard_map/output_projection/pallas_call | solution.py:258
  235.7 1.1 convert_element_type.46
  236.9 0.7 pad_maximum_fusion.5
  237.6 0.7 collective-permute-done.27
  238.3 0.7 fusion
  (67 shorter events, 5.3 us)
Async XLA Ops:
  4.9 20.1 %collective-permute-start = (bf16[256,1024]{1,0:T(8,128)(2,1)}, bf16[256,1024]{1,0:T(8,128)(2,1)}, u32[]{:S(2)}, u32[]{:S(2)}) collective-permute-start(bf16[256,1024]{1,0:T(8,128)(2,1)} %query_projection.5), channel_id=1, source_target_pairs={{0,2},{2,0},{4,6},{6,4},{8,10},{10,8},{12,14},{14,12},{16,18},{18,... | collective-permute-start | bytes 1572872 | tf_op jit(solution)/shard_map/ppermute | solution.py:29
  10.4 24.9 %collective-permute-start.1 = (bf16[256,1024]{1,0:T(8,128)(2,1)}, bf16[256,1024]{1,0:T(8,128)(2,1)}, u32[]{:S(2)}, u32[]{:S(2)}) collective-permute-start(bf16[256,1024]{1,0:T(8,128)(2,1)} %query_projection.6), channel_id=1, source_target_pairs={{0,4},{2,6},{4,0},{6,2},{8,12},{10,14},{12,8},{14,10},{16,20},{18,... | collective-permute-start | bytes 1572872 | tf_op jit(solution)/shard_map/ppermute | solution.py:29
  14.5 20.9 %collective-permute-start.2 = (bf16[256,1024]{1,0:T(8,128)(2,1)}, bf16[256,1024]{1,0:T(8,128)(2,1)}, u32[]{:S(2)}, u32[]{:S(2)}) collective-permute-start(bf16[256,1024]{1,0:T(8,128)(2,1)} %query_projection.7), channel_id=1, source_target_pairs={{0,6},{2,4},{4,2},{6,0},{8,14},{10,12},{12,10},{14,8},{16,22},{18,... | collective-permute-start | bytes 1572872 | tf_op jit(solution)/shard_map/ppermute | solution.py:29
  14.5 2.9 %copy-start.2 = (bf16[4,2048,128]{2,1,0:T(8,128)(2,1)S(1)}, bf16[4,2048,128]{2,1,0:T(8,128)(2,1)}, u32[]{:S(2)}) copy-start(bf16[4,2048,128]{2,1,0:T(8,128)(2,1)} %param.10) | copy-start | bytes 6291460
  20.6 3.3 %copy-start.3 = (bf16[4,2048,128]{2,1,0:T(8,128)(2,1)S(1)}, bf16[4,2048,128]{2,1,0:T(8,128)(2,1)}, u32[]{:S(2)}) copy-start(bf16[4,2048,128]{2,1,0:T(8,128)(2,1)} %param.9) | copy-start | bytes 6291460
  23.8 11.5 %copy-start = (f32[256,1024]{1,0:T(8,128)S(1)}, f32[256,1024]{1,0:T(8,128)}, u32[]{:S(2)}) copy-start(f32[256,1024]{1,0:T(8,128)} %query_projection.4) | copy-start | bytes 3145732
  37.1 20.9 %copy-start.10 = (bf16[1,4,512,128]{2,3,1,0:T(8,128)(2,1)S(1)}, bf16[1,4,512,128]{2,3,1,0:T(8,128)(2,1)}, u32[]{:S(2)}) copy-start(bf16[1,4,512,128]{2,3,1,0:T(8,128)(2,1)} %copy.13) | copy-start | bytes 1572868
  37.1 28.1 %copy-start.9 = (bf16[1,4,512,128]{2,3,1,0:T(8,128)(2,1)S(1)}, bf16[1,4,512,128]{2,3,1,0:T(8,128)(2,1)}, u32[]{:S(2)}) copy-start(bf16[1,4,512,128]{2,3,1,0:T(8,128)(2,1)} %copy.14) | copy-start | bytes 1572868
  37.1 29.0 %copy-start.8 = (bf16[1,4,512,128]{2,3,1,0:T(8,128)(2,1)S(1)}, bf16[1,4,512,128]{2,3,1,0:T(8,128)(2,1)}, u32[]{:S(2)}) copy-start(bf16[1,4,512,128]{2,3,1,0:T(8,128)(2,1)} %copy.15) | copy-start | bytes 1572868
  37.2 30.1 %collective-permute-start.10 = (bf16[2048,128]{1,0:T(8,128)(2,1)}, bf16[2048,128]{1,0:T(8,128)(2,1)}, u32[]{:S(2)}, u32[]{:S(2)}) collective-permute-start(bf16[2048,128]{1,0:T(8,128)(2,1)} %get-tuple-element.11), channel_id=1, source_target_pairs={{0,4},{2,6},{4,0},{6,2},{8,12},{10,14},{12,8},{14,10},{16,20},{18,... | collective-permute-start | bytes 1572872 | tf_op jit(solution)/shard_map/ppermute | solution.py:29
  38.8 6.1 %collective-permute-start.3 = (bf16[64,1024]{1,0:T(8,128)(2,1)S(1)}, bf16[64,1024]{1,0:T(8,128)(2,1)S(1)}, u32[]{:S(2)}, u32[]{:S(2)}) collective-permute-start(bf16[64,1024]{1,0:T(8,128)(2,1)S(1)} %get-tuple-element.30), channel_id=1, source_target_pairs={{0,8},{2,10},{4,12},{6,14},{8,0},{10,2},{12,4},{14,6},{16,24},{18,... | collective-permute-start | bytes 393224 | tf_op jit(solution)/shard_map/ppermute | solution.py:29
  40.4 11.5 %collective-permute-start.4 = (bf16[64,1024]{1,0:T(8,128)(2,1)S(1)}, bf16[64,1024]{1,0:T(8,128)(2,1)S(1)}, u32[]{:S(2)}, u32[]{:S(2)}) collective-permute-start(bf16[64,1024]{1,0:T(8,128)(2,1)S(1)} %get-tuple-element.32), channel_id=1, source_target_pairs={{0,16},{2,18},{4,20},{6,22},{8,24},{10,26},{12,28},{14,30},{16,0},... | collective-permute-start | bytes 393224 | tf_op jit(solution)/shard_map/ppermute | solution.py:29
  43.0 8.9 %collective-permute-start.5 = (bf16[64,1024]{1,0:T(8,128)(2,1)S(1)}, bf16[64,1024]{1,0:T(8,128)(2,1)S(1)}, u32[]{:S(2)}, u32[]{:S(2)}) collective-permute-start(bf16[64,1024]{1,0:T(8,128)(2,1)S(1)} %get-tuple-element.31), channel_id=1, source_target_pairs={{0,24},{2,26},{4,28},{6,30},{8,16},{10,18},{12,20},{14,22},{16,8},... | collective-permute-start | bytes 393224 | tf_op jit(solution)/shard_map/ppermute | solution.py:29
  52.0 6.1 %collective-permute-start.6 = (bf16[64,1024]{1,0:T(8,128)(2,1)S(1)}, bf16[64,1024]{1,0:T(8,128)(2,1)S(1)}, u32[]{:S(2)}, u32[]{:S(2)}) collective-permute-start(bf16[64,1024]{1,0:T(8,128)(2,1)S(1)} %add_convert_fusion), channel_id=1, source_target_pairs={{0,8},{2,10},{4,12},{6,14},{8,0},{10,2},{12,4},{14,6},{16,24},{18,... | collective-permute-start | bytes 393224 | tf_op jit(solution)/shard_map/ppermute | solution.py:29
  54.0 11.2 %collective-permute-start.7 = (bf16[64,1024]{1,0:T(8,128)(2,1)S(1)}, bf16[64,1024]{1,0:T(8,128)(2,1)S(1)}, u32[]{:S(2)}, u32[]{:S(2)}) collective-permute-start(bf16[64,1024]{1,0:T(8,128)(2,1)S(1)} %add_convert_fusion), channel_id=1, source_target_pairs={{0,16},{2,18},{4,20},{6,22},{8,24},{10,26},{12,28},{14,30},{16,0},... | collective-permute-start | bytes 393224 | tf_op jit(solution)/shard_map/ppermute | solution.py:29
  55.1 11.0 %collective-permute-start.8 = (bf16[64,1024]{1,0:T(8,128)(2,1)S(1)}, bf16[64,1024]{1,0:T(8,128)(2,1)S(1)}, u32[]{:S(2)}, u32[]{:S(2)}) collective-permute-start(bf16[64,1024]{1,0:T(8,128)(2,1)S(1)} %add_convert_fusion), channel_id=1, source_target_pairs={{0,24},{2,26},{4,28},{6,30},{8,16},{10,18},{12,20},{14,22},{16,8},... | collective-permute-start | bytes 393224 | tf_op jit(solution)/shard_map/ppermute | solution.py:29
  57.2 16.1 %collective-permute-start.11 = (bf16[2048,128]{1,0:T(8,128)(2,1)}, bf16[2048,128]{1,0:T(8,128)(2,1)}, u32[]{:S(2)}, u32[]{:S(2)}) collective-permute-start(bf16[2048,128]{1,0:T(8,128)(2,1)} %get-tuple-element.12), channel_id=1, source_target_pairs={{0,6},{2,4},{4,2},{6,0},{8,14},{10,12},{12,10},{14,8},{16,22},{18,... | collective-permute-start | bytes 1572872 | tf_op jit(solution)/shard_map/ppermute | solution.py:29
  58.0 25.6 %collective-permute-start.12 = (bf16[4,128,512]{2,1,0:T(8,128)(2,1)S(1)}, bf16[4,128,512]{2,1,0:T(8,128)(2,1)}, u32[]{:S(2)}, u32[]{:S(2)}) collective-permute-start(bf16[4,128,512]{2,1,0:T(8,128)(2,1)S(1)} %bitcast.83), channel_id=1, source_target_pairs={{0,2},{2,0},{4,6},{6,4},{8,10},{10,8},{12,14},{14,12},{16,18},{18,... | collective-permute-start | bytes 1572872 | tf_op jit(solution)/shard_map/ppermute | solution.py:29
  65.2 19.3 %collective-permute-start.13 = (bf16[4,128,512]{2,1,0:T(8,128)(2,1)S(1)}, bf16[4,128,512]{2,1,0:T(8,128)(2,1)}, u32[]{:S(2)}, u32[]{:S(2)}) collective-permute-start(bf16[4,128,512]{2,1,0:T(8,128)(2,1)S(1)} %bitcast.82), channel_id=1, source_target_pairs={{0,4},{2,6},{4,0},{6,2},{8,12},{10,14},{12,8},{14,10},{16,20},{18,... | collective-permute-start | bytes 1572872 | tf_op jit(solution)/shard_map/ppermute | solution.py:29
  66.1 29.7 %collective-permute-start.14 = (bf16[4,128,512]{2,1,0:T(8,128)(2,1)S(1)}, bf16[4,128,512]{2,1,0:T(8,128)(2,1)}, u32[]{:S(2)}, u32[]{:S(2)}) collective-permute-start(bf16[4,128,512]{2,1,0:T(8,128)(2,1)S(1)} %bitcast.81), channel_id=1, source_target_pairs={{0,6},{2,4},{4,2},{6,0},{8,14},{10,12},{12,10},{14,8},{16,22},{18,... | collective-permute-start | bytes 1572872 | tf_op jit(solution)/shard_map/ppermute | solution.py:29
  67.2 36.0 %collective-permute-start.9 = (bf16[2048,128]{1,0:T(8,128)(2,1)S(1)}, bf16[2048,128]{1,0:T(8,128)(2,1)}, u32[]{:S(2)}, u32[]{:S(2)}) collective-permute-start(bf16[2048,128]{1,0:T(8,128)(2,1)S(1)} %get-tuple-element.10), channel_id=1, source_target_pairs={{0,2},{2,0},{4,6},{6,4},{8,10},{10,8},{12,14},{14,12},{16,18},{18,... | collective-permute-start | bytes 1572872 | tf_op jit(solution)/shard_map/ppermute | solution.py:29
  165.7 7.5 %collective-permute-start.15 = (bf16[64,1152]{1,0:T(8,128)(2,1)S(1)}, bf16[64,1152]{1,0:T(8,128)(2,1)S(1)}, u32[]{:S(2)}, u32[]{:S(2)}) collective-permute-start(bf16[64,1152]{1,0:T(8,128)(2,1)S(1)} %get-tuple-element.28), channel_id=1, source_target_pairs={{0,8},{2,10},{4,12},{6,14},{8,0},{10,2},{12,4},{14,6},{16,24},{18,... | collective-permute-start | bytes 442376 | tf_op jit(solution)/shard_map/ppermute | solution.py:29
  166.5 10.8 %collective-permute-start.16 = (bf16[64,1152]{1,0:T(8,128)(2,1)S(1)}, bf16[64,1152]{1,0:T(8,128)(2,1)S(1)}, u32[]{:S(2)}, u32[]{:S(2)}) collective-permute-start(bf16[64,1152]{1,0:T(8,128)(2,1)S(1)} %get-tuple-element.27), channel_id=1, source_target_pairs={{0,16},{2,18},{4,20},{6,22},{8,24},{10,26},{12,28},{14,30},{16,0},... | collective-permute-start | bytes 442376 | tf_op jit(solution)/shard_map/ppermute | solution.py:29
  166.5 10.8 %collective-permute-start.17 = (bf16[64,1152]{1,0:T(8,128)(2,1)S(1)}, bf16[64,1152]{1,0:T(8,128)(2,1)S(1)}, u32[]{:S(2)}, u32[]{:S(2)}) collective-permute-start(bf16[64,1152]{1,0:T(8,128)(2,1)S(1)} %get-tuple-element.26), channel_id=1, source_target_pairs={{0,24},{2,26},{4,28},{6,30},{8,16},{10,18},{12,20},{14,22},{16,8},... | collective-permute-start | bytes 442376 | tf_op jit(solution)/shard_map/ppermute | solution.py:29
  173.2 4.0 %copy-start.11 = (bf16[64,1152]{1,0:T(8,128)(2,1)}, bf16[64,1152]{1,0:T(8,128)(2,1)S(1)}, u32[]{:S(2)}) copy-start(bf16[64,1152]{1,0:T(8,128)(2,1)S(1)} %collective-permute-done.15.refs_1_) | copy-start | bytes 442372
  177.3 0.7 copy-start.12
  177.3 0.7 copy-start.13
  180.2 7.2 %collective-permute-start.18 = (bf16[64,1152]{1,0:T(8,128)(2,1)}, bf16[64,1152]{1,0:T(8,128)(2,1)S(1)}, u32[]{:S(2)}, u32[]{:S(2)}) collective-permute-start(bf16[64,1152]{1,0:T(8,128)(2,1)} %merge.1), channel_id=1, source_target_pairs={{0,8},{2,10},{4,12},{6,14},{8,0},{10,2},{12,4},{14,6},{16,24},{18,... | collective-permute-start | bytes 442376 | tf_op jit(solution)/shard_map/ppermute | solution.py:29
  182.9 12.6 %collective-permute-start.19 = (bf16[64,1152]{1,0:T(8,128)(2,1)}, bf16[64,1152]{1,0:T(8,128)(2,1)S(1)}, u32[]{:S(2)}, u32[]{:S(2)}) collective-permute-start(bf16[64,1152]{1,0:T(8,128)(2,1)} %merge.1), channel_id=1, source_target_pairs={{0,16},{2,18},{4,20},{6,22},{8,24},{10,26},{12,28},{14,30},{16,0},... | collective-permute-start | bytes 442376 | tf_op jit(solution)/shard_map/ppermute | solution.py:29
  182.9 12.6 %collective-permute-start.20 = (bf16[64,1152]{1,0:T(8,128)(2,1)}, bf16[64,1152]{1,0:T(8,128)(2,1)S(1)}, u32[]{:S(2)}, u32[]{:S(2)}) collective-permute-start(bf16[64,1152]{1,0:T(8,128)(2,1)} %merge.1), channel_id=1, source_target_pairs={{0,24},{2,26},{4,28},{6,30},{8,16},{10,18},{12,20},{14,22},{16,8},... | collective-permute-start | bytes 442376 | tf_op jit(solution)/shard_map/ppermute | solution.py:29
  196.5 3.6 %copy-start.1 = (bf16[256,1152]{1,0:T(8,128)(2,1)}, bf16[256,1152]{1,0:T(8,128)(2,1)S(1)}, u32[]{:S(2)}) copy-start(bf16[256,1152]{1,0:T(8,128)(2,1)S(1)} %pad_maximum_fusion.a_ref) | copy-start | bytes 1769476
  196.5 19.1 %copy-start.4 = (bf16[256,1024]{1,0:T(8,128)(2,1)}, bf16[256,1024]{1,0:T(8,128)(2,1)S(1)}, u32[]{:S(2)}) copy-start(bf16[256,1024]{1,0:T(8,128)(2,1)S(1)} %slice.24.a_ref) | copy-start | bytes 1572868
  196.5 28.4 %collective-permute-start.26 = (bf16[256,1024]{1,0:T(8,128)(2,1)S(1)}, bf16[256,1024]{1,0:T(8,128)(2,1)S(1)}, u32[]{:S(2)}, u32[]{:S(2)}) collective-permute-start(bf16[256,1024]{1,0:T(8,128)(2,1)S(1)} %slice.24.a_ref), channel_id=1, source_target_pairs={{0,2},{2,0},{4,6},{6,4},{8,10},{10,8},{12,14},{14,12},{16,18},{18,... | collective-permute-start | bytes 1572872 | tf_op jit(solution)/shard_map/ppermute | solution.py:29
  197.1 31.4 %collective-permute-start.25 = (bf16[256,1024]{1,0:T(8,128)(2,1)S(1)}, bf16[256,1024]{1,0:T(8,128)(2,1)S(1)}, u32[]{:S(2)}, u32[]{:S(2)}) collective-permute-start(bf16[256,1024]{1,0:T(8,128)(2,1)S(1)} %slice.24.a_ref), channel_id=1, source_target_pairs={{0,4},{2,6},{4,0},{6,2},{8,12},{10,14},{12,8},{14,10},{16,20},{18,... | collective-permute-start | bytes 1572872 | tf_op jit(solution)/shard_map/ppermute | solution.py:29
  197.5 34.6 %collective-permute-start.24 = (bf16[256,1024]{1,0:T(8,128)(2,1)S(1)}, bf16[256,1024]{1,0:T(8,128)(2,1)S(1)}, u32[]{:S(2)}, u32[]{:S(2)}) collective-permute-start(bf16[256,1024]{1,0:T(8,128)(2,1)S(1)} %slice.24.a_ref), channel_id=1, source_target_pairs={{0,6},{2,4},{4,2},{6,0},{8,14},{10,12},{12,10},{14,8},{16,22},{18,... | collective-permute-start | bytes 1572872 | tf_op jit(solution)/shard_map/ppermute | solution.py:29
  216.4 3.9 %collective-permute-start.21 = (f32[1,2048]{1,0:T(1,128)S(1)}, f32[1,2048]{1,0:T(1,128)S(1)}, u32[]{:S(2)}, u32[]{:S(2)}) collective-permute-start(f32[1,2048]{1,0:T(1,128)S(1)} %bitcast.89), channel_id=1, source_target_pairs={{0,2},{2,0},{4,6},{6,4},{8,10},{10,8},{12,14},{14,12},{16,18},{18,... | collective-permute-start | bytes 24584 | tf_op jit(solution)/shard_map/ppermute | solution.py:29
  217.0 6.2 %collective-permute-start.22 = (f32[1,2048]{1,0:T(1,128)S(1)}, f32[1,2048]{1,0:T(1,128)S(1)}, u32[]{:S(2)}, u32[]{:S(2)}) collective-permute-start(f32[1,2048]{1,0:T(1,128)S(1)} %bitcast.87), channel_id=1, source_target_pairs={{0,4},{2,6},{4,0},{6,2},{8,12},{10,14},{12,8},{14,10},{16,20},{18,... | collective-permute-start | bytes 24584 | tf_op jit(solution)/shard_map/ppermute | solution.py:29
  220.3 4.5 %collective-permute-start.23 = (f32[1,2048]{1,0:T(1,128)S(1)}, f32[1,2048]{1,0:T(1,128)S(1)}, u32[]{:S(2)}, u32[]{:S(2)}) collective-permute-start(f32[1,2048]{1,0:T(1,128)S(1)} %bitcast.88), channel_id=1, source_target_pairs={{0,6},{2,4},{4,2},{6,0},{8,14},{10,12},{12,10},{14,8},{16,22},{18,... | collective-permute-start | bytes 24584 | tf_op jit(solution)/shard_map/ppermute | solution.py:29
  224.9 0.8 copy-start.7
  228.5 0.8 copy-start.6
  232.1 0.8 copy-start.5
  236.8 1.4 collective-permute-start.27
